TPU v7x, 32 devices: a whole 2x2x4 slice. The times are simulated.
32 devices in a mesh: day: 8 (over z, x), blk: 4 (over y, core).
Axes of the slice: x: 2, y: 2, z: 4, core: 2. Of those that a mesh axis runs over, the one named last changes fastest.
Arguments:
- diag_blocks: float32 [16, 2560, 2560], P('day', 'blk'), may hold values from -1 to 3, as said below
- off_blocks: float32 [16, 2560, 2560], P('day', 'blk'), may hold values from -1 to 1
- leakage: float32 [16, 2560], P('day', 'blk'), may hold values from 0.001 to 0.3
- obs_count: int32 [16], P('day'), may hold values from 1 to 1024, 8192 in all
- obs_triangle: int32 [16, 1024], P('day', 'blk'), may hold values from 0 to 5115
- obs_bary: float32 [3, 16, 1024], P(None, 'day', 'blk'), may hold values from 0.05 to 1
- obs_prec: float32 [16, 1024], P('day', 'blk'), may hold values from 0.3 to 3
- obs_value: float32 [16, 1024], P('day', 'blk'), may hold values from -6 to 6
- covariates: float32 [64, 16, 1024], P(None, 'day', 'blk'), may hold values from -0.09375 to 0.09375
- triangles: int32 [3, 5116], replicated, may hold values from 0 to 2559
- prior_prec: float32 [64], replicated, may hold values from 0.5 to 2
- probes: float32 [15, 16, 2560], P(None, 'day', 'blk'), may hold values from -6 to 6
- probes_cov: float32 [15, 64], replicated, may hold values from -6 to 6
Outputs:
- step_field: float32 [16, 16, 2560], P(None, 'day', 'blk')
- step_cov: float32 [16, 64], replicated
Inputs may be any that keep to these rules, and one draw needn't show every extreme that they name: Every block diag_blocks[t] is symmetric, and the whole precision made of diag_blocks and off_blocks is positive definite. Slots 0 to obs_count[t] - 1 of day t hold observations, the others are empty; the counts sum to 8192.
All inputs are finite; a program needn't handle non-finite values. No bound on the sum of `obs_count` on one device may be relied on, other than what follows from the above.
Results may differ from a plain program's by a relative error of at most 0.0002.
Values sent between devices are 32-bit elements; how exact they have to be, the bound alone decides.
A program may use at most 192 MiB of HBM per device.

v0:
```python
import jax
import jax.numpy as jnp
from jax import lax
from jax.sharding import PartitionSpec as P

ITERS = 3


exact_precision = lax.Precision.HIGHEST


def prefix(part, axis, combine, identity, reverse):
    count = lax.axis_size(axis)
    place = lax.axis_index(axis)
    ahead = count - 1 - place if reverse else place
    gathered = jax.tree.map(lambda a: lax.all_gather(a, axis), part)
    state = jax.tree.map(lambda a, e: jnp.zeros_like(a) + jnp.asarray(e, a.dtype), part, identity)

    def one(turn, state):
        source = count - 1 - turn if reverse else turn
        return combine(
            state, jax.tree.map(lambda a: lax.dynamic_index_in_dim(a, source, 0, False), gathered)
        )

    return lax.fori_loop(0, ahead, one, state)


def shifted(block, axis, distance):
    devices = range(lax.axis_size(axis))
    route = [(i - distance, i) for i in devices if i - distance in devices]
    return lax.ppermute(block, axis, route)


def spread(values, flat_ids, segments):
    leading = values.shape[0]
    summed = jax.ops.segment_sum(values.reshape(leading, -1).T, flat_ids, num_segments=segments)
    return summed.T


def chain_combine(earlier, later):
    return (earlier[0] * later[0], later[0] * earlier[1] + later[1])


def precondition(residual, decays, dominant):
    day_count = decays.shape[0]
    running = jnp.zeros_like(residual[:, 0])
    factor = jnp.ones_like(decays[0])
    partials = []
    factors = []
    for index_day in range(day_count):
        running = residual[:, index_day] + decays[index_day] * running
        factor = factor * decays[index_day]
        partials.append(running)
        factors.append(factor)
    incoming = prefix(
        (factor, running),
        "day",
        chain_combine,
        (jnp.ones_like(factor), jnp.zeros_like(running)),
        False,
    )[1]
    scaled = [
        (partials[index_day] + factors[index_day] * incoming) / dominant[index_day]
        for index_day in range(day_count)
    ]
    backward_values = [None] * day_count
    tail_factors = [None] * day_count
    running = jnp.zeros_like(incoming)
    tail_factor = jnp.ones_like(factor)
    for index_day in range(day_count - 1, -1, -1):
        if index_day + 1 < day_count:
            running = scaled[index_day] + decays[index_day + 1] * running
            tail_factor = tail_factor * decays[index_day + 1]
        else:
            running = scaled[index_day]
        backward_values[index_day] = running
        tail_factors[index_day] = tail_factor
    upward = prefix(
        (factor, decays[0] * backward_values[0]),
        "day",
        chain_combine,
        (jnp.ones_like(factor), jnp.zeros_like(running)),
        True,
    )[1]
    return jnp.stack(
        [
            backward_values[index_day] + tail_factors[index_day] * upward
            for index_day in range(day_count)
        ],
        axis=1,
    )


def on_device(
    diag_blocks,
    off_blocks,
    leakage,
    obs_count,
    obs_triangle,
    obs_bary,
    obs_prec,
    obs_value,
    covariates,
    triangles,
    prior_prec,
    probes,
    probes_cov,
):
    day_count, row_count, node_count = diag_blocks.shape
    slot_count = obs_triangle.shape[1]
    row_start = lax.axis_index("blk") * row_count
    slot_start = lax.axis_index("blk") * slot_count
    slot_index = lax.broadcasted_iota(jnp.int32, obs_triangle.shape, 1) + slot_start
    slot_weight = jnp.where(slot_index < obs_count[:, None], obs_prec, jnp.zeros_like(obs_prec))
    vertices = triangles[:, obs_triangle]
    day_index = lax.broadcasted_iota(jnp.int32, vertices.shape, 1)
    flat_ids = (vertices + node_count * day_index).reshape(-1)
    barycentric = obs_bary / jnp.sum(obs_bary, axis=0, keepdims=True)
    segments = day_count * node_count
    decays = 1.0 - leakage
    dominant = jnp.diagonal(
        lax.dynamic_slice_in_dim(diag_blocks, row_start, row_count, 2), axis1=1, axis2=2
    )

    def inner_norm(residual, preconditioned, residual_cov):
        summed = lax.psum(jnp.sum(residual * preconditioned, axis=(1, 2)), ("day", "blk"))
        return summed + jnp.sum(residual_cov * residual_cov, axis=1)

    weighted_value = slot_weight * obs_value
    grad_terms = spread((barycentric * weighted_value[None])[None], flat_ids, segments).reshape(
        1, day_count, node_count
    )
    grad_field = lax.psum_scatter(grad_terms, "blk", scatter_dimension=2, tiled=True)
    grad_cov = lax.psum(
        jnp.einsum("ctj,tj->c", covariates, weighted_value, precision=exact_precision),
        ("day", "blk"),
    )
    residual = jnp.concatenate([grad_field, probes], axis=0)
    residual_cov = jnp.concatenate([grad_cov[None], probes_cov], axis=0)
    solution = jnp.zeros_like(residual)
    solution_cov = jnp.zeros_like(residual_cov)
    preconditioned = precondition(residual, decays, dominant)
    direction = preconditioned
    direction_cov = residual_cov
    norm_now = inner_norm(residual, preconditioned, residual_cov)
    for iteration in range(ITERS):
        rhs_count = direction.shape[0]
        gathered = lax.all_gather(direction, "blk", axis=2, tiled=True)
        arriving = shifted(gathered[:, 0], "day", -1)
        following = jnp.concatenate([gathered[:, 1:], arriving[:, None]], axis=1)
        diagonal_terms = jnp.einsum(
            "tis,rts->rti", diag_blocks, gathered, precision=exact_precision
        )
        ahead_terms = jnp.einsum("tis,rts->rti", off_blocks, following, precision=exact_precision)
        behind_terms = jnp.einsum("tis,rti->rts", off_blocks, direction, precision=exact_precision)
        picked = gathered.reshape(rhs_count, -1)[:, flat_ids].reshape(
            (rhs_count,) + barycentric.shape
        )
        predictor = jnp.sum(barycentric[None] * picked, axis=1) + jnp.einsum(
            "ctj,rc->rtj", covariates, direction_cov, precision=exact_precision
        )
        weighted = slot_weight[None] * predictor
        obs_terms = spread(barycentric[None] * weighted[:, None], flat_ids, segments).reshape(
            rhs_count, day_count, node_count
        )
        cov_terms = jnp.einsum("ctj,rtj->rc", covariates, weighted, precision=exact_precision)
        arrived = shifted(behind_terms[:, -1], "day", 1)
        earlier = jnp.concatenate([arrived[:, None], behind_terms[:, :-1]], axis=1)
        reduced = lax.psum_scatter(obs_terms + earlier, "blk", scatter_dimension=2, tiled=True)
        image, cov_terms = (diagonal_terms + ahead_terms + reduced, cov_terms)
        local_curve = jnp.sum(direction * image, axis=(1, 2)) + jnp.sum(
            direction_cov * cov_terms, axis=1
        )
        cov_total, curve_total = lax.psum((cov_terms, local_curve), ("day", "blk"))
        image_cov = cov_total + prior_prec[None] * direction_cov
        curvature = curve_total + jnp.sum(direction_cov * prior_prec[None] * direction_cov, axis=1)
        step_length = norm_now / curvature
        solution = solution + step_length[:, None, None] * direction
        solution_cov = solution_cov + step_length[:, None] * direction_cov
        if iteration + 1 < ITERS:
            residual = residual - step_length[:, None, None] * image
            residual_cov = residual_cov - step_length[:, None] * image_cov
            preconditioned = precondition(residual, decays, dominant)
            norm_next = inner_norm(residual, preconditioned, residual_cov)
            conjugacy = norm_next / norm_now
            direction = preconditioned + conjugacy[:, None, None] * direction
            direction_cov = residual_cov + conjugacy[:, None] * direction_cov
            norm_now = norm_next
    return (solution, solution_cov)


def solution(mesh):
    in_specs = (
        P("day", "blk", None),
        P("day", "blk", None),
        P("day", "blk"),
        P("day"),
        P("day", "blk"),
        P(None, "day", "blk"),
        P("day", "blk"),
        P("day", "blk"),
        P(None, "day", "blk"),
        P(),
        P(),
        P(None, "day", "blk"),
        P(),
    )
    out_specs = (P(None, "day", "blk"), P())
    return jax.shard_map(
        on_device, mesh=mesh, in_specs=in_specs, out_specs=out_specs, check_vma=False
    )
```

profile of v0, /device:TPU:0, one launch (start us, length us, event | category | flops | bytes accessed | tf_op | source)
XLA Modules:
  0.0 756.4 jit_solution(16778236442979294471)
XLA Ops:
  13.7 8.6 %scatter_custom_fusion = f32[5120]{0:T(1024)S(1)} fusion(s32[1536]{0:T(1024)S(1)} %reshape.352, f32[1536]{0:T(1024)S(1)} %reshape.354, f32[]{:T(128)} %constant.153.clone.1), kind=kCustom, calls=%fused_computation.149 | custom fusion | flops 1536 | bytes 20484 | tf_op jit(solution)/shard_map/scatter-add | solution.py:36
  23.6 14.3 %bitcast_reduce_fusion = f32[2560,2]{1,0:T(8,128)} fusion(f32[1,2,2560]{0,1,2:T(2,128)S(1)} %copy.93), kind=kLoop, calls=%fused_computation.24 | loop fusion | bytes 40960
  38.0 2.1 constant_dynamic-slice_fusion
  40.2 2.5 copy.99
  42.7 4.6 gather_fusion.1
  47.6 32.3 %all-gather.3 = f32[8,1,640]{2,1,0:T(1,128)S(1)} all-gather(f32[1,1,640]{2,1,0:T(1,128)S(1)} %get-tuple-element.515), channel_id=1, replica_groups=mesh['day'=8,'blk'=4] {'day'}, dimensions={0}, use_global_device_ids=true | all-gather | bytes 23040 | tf_op jit(solution)/shard_map/all_gather | solution.py:16
  80.0 39.5 %psum.64 = f32[1,64]{1,0:T(1,128)S(1)} all-reduce(f32[1,64]{1,0:T(1,128)S(1)} %convolution_bitcast_fusion.6), channel_id=1, replica_groups=mesh['day'=8,'blk'=4] {'day','blk'}, use_global_device_ids=true, to_apply=%region_9.10 | all-reduce | flops 64 | bytes 512 | tf_op jit(solution)/shard_map/psum | solution.py:134
  119.4 1.7 reshape_bitcast_fusion
  121.5 31.0 %all_gather.54 = f32[8,16,640]{2,1,0:T(8,128)S(1)} all-gather(f32[1,16,640]{2,1,0:T(8,128)S(1)} %fusion.51), channel_id=1, replica_groups=mesh['day'=8,'blk'=4] {'day'}, dimensions={0}, use_global_device_ids=true | all-gather | bytes 368640 | tf_op jit(solution)/shard_map/all_gather | solution.py:16
  152.5 30.9 %all-gather = f32[128,640]{1,0:T(8,128)S(1)} all-gather(f32[16,640]{1,0:T(8,128)S(1)} %get-tuple-element.490), channel_id=2, replica_groups=mesh['day'=8,'blk'=4] {'day'}, dimensions={0}, use_global_device_ids=true | all-gather | bytes 368640 | tf_op jit(solution)/shard_map/all_gather | solution.py:16
  183.9 7.0 all_gather.57
  192.4 3.7 gather_fusion.2
  197.5 9.2 %convolution_bitcast_fusion.2 = f32[16,2,2560]{2,0,1:T(8,128)S(1)} fusion(f32[2,640,2560]{2,1,0:T(8,128)} %param.26, f32[16,1,640]{2,0,1:T(8,128)S(1)} %get-tuple-element.514, f32[16,1,640]{2,0,1:T(8,128)S(1)} %get-tuple-element.513), kind=kOutput, calls=%fused_computation.23 | convolution fusion | flops 629166080 | bytes 13516800 | tf_op jit(solution)/shard_map/tis,rti->rts/dot_general | solution.py:155
  207.5 2.6 collective-permute-start.1
  211.6 9.0 %scatter_custom_fusion.1 = f32[5120,16]{1,0:T(8,128)S(1)} fusion(s32[1536]{0:T(1024)} %copy-done.35, f32[]{:T(128)} %constant.153.clone.1, f32[16,1536]{0,1:T(8,128)} %bitcast_multiply_fusion.2), kind=kCustom, calls=%fused_computation.29 | custom fusion | flops 24576 | bytes 1114624 | tf_op jit(solution)/shard_map/scatter-add | solution.py:36
  223.3 1.8 maximum_add_fusion
  225.4 13.6 %fusion.80 = f32[2,16,640]{2,1,0:T(8,128)S(1)} fusion(f32[16,2,2560]{2,0,1:T(8,128)S(1)} %all_gather.57, f32[2,640,2560]{2,1,0:T(8,128)} %param.25), kind=kOutput, calls=%fused_computation.205 | convolution fusion | flops 629145600 | bytes 13516800 | tf_op jit(solution)/shard_map/tis,rts->rti/dot_general | solution.py:151
  239.3 6.5 reduce-scatter.7.cloned.1.call-done
  245.9 13.8 %multiply_reduce_fusion.6 = (f32[16]{0:T(128)S(1)}, f32[16]{0:T(128)S(1)}, f32[16,2,640]{2,0,1:T(8,128)S(1)}) fusion(f32[16,1,640]{2,0,1:T(8,128)S(1)} %get-tuple-element.514, f32[16,1,640]{2,0,1:T(8,128)S(1)} %get-tuple-element.513, f32[15,2,640]{2,0,1:T(8,128)S(1)} %copy.56, f32[1,2,640]{2,0,1:T(1,128)S(1)} %copy.94, ...), kind=kOutput, calls=%fused_computation.103 | convolution fusion | flops 629391360 | bytes 13844608 | tf_op jit(solution)/shard_map/tis,rts->rti/dot_general | solution.py:154
  259.7 39.3 %all-reduce.2 = (f32[16]{0:T(128)S(1)}, f32[16]{0:T(128)S(1)}) all-reduce(f32[16]{0:T(128)S(1)} %get-tuple-element.399, f32[16]{0:T(128)S(1)} %add.435), channel_id=1, replica_groups=mesh['day'=8,'blk'=4] {'day','blk'}, use_global_device_ids=true, to_apply=%region_8.9 | all-reduce | flops 32 | bytes 256 | tf_op jit(solution)/shard_map/psum | solution.py:126
  299.8 30.9 %all_gather.58 = f32[8,16,640]{2,1,0:T(8,128)S(1)} all-gather(f32[1,16,640]{2,1,0:T(8,128)S(1)} %fusion.47), channel_id=1, replica_groups=mesh['day'=8,'blk'=4] {'day'}, dimensions={0}, use_global_device_ids=true | all-gather | bytes 368640 | tf_op jit(solution)/shard_map/all_gather | solution.py:16
  330.8 30.9 %all-gather.1 = f32[128,640]{1,0:T(8,128)S(1)} all-gather(f32[16,640]{1,0:T(8,128)S(1)} %get-tuple-element.486), channel_id=3, replica_groups=mesh['day'=8,'blk'=4] {'day'}, dimensions={0}, use_global_device_ids=true | all-gather | bytes 368640 | tf_op jit(solution)/shard_map/all_gather | solution.py:16
  362.4 39.5 %all-reduce.1 = (f32[16]{0:T(128)S(1)}, f32[16,64]{1,0:T(8,128)S(1)}) all-reduce(f32[16]{0:T(128)S(1)} %multiply_reduce_fusion.5, f32[16,64]{1,0:T(8,128)S(1)} %get-tuple-element.517), channel_id=1, replica_groups=mesh['day'=8,'blk'=4] {'day','blk'}, use_global_device_ids=true, to_apply=%region_23.24 | all-reduce | flops 1040 | bytes 8320 | tf_op jit(solution)/shard_map/psum | solution.py:126
  402.7 7.3 all_gather.61
  410.0 11.4 %convolution_bitcast_fusion.1 = f32[16,2,2560]{2,0,1:T(8,128)} fusion(f32[16,2,640]{2,0,1:T(8,128)S(1)} %multiply_add_fusion.2, f32[2,640,2560]{2,1,0:T(8,128)} %param.26), kind=kOutput, calls=%fused_computation.22 | convolution fusion | flops 629145600 | bytes 13516800 | tf_op jit(solution)/shard_map/tis,rti->rts/dot_general | solution.py:155
  423.0 3.7 gather_fusion.3
  428.2 1.7 slice_bitcast_fusion.2
  430.0 3.9 collective-permute-start.3
  436.0 9.0 %scatter_custom_fusion.2 = f32[5120,16]{1,0:T(8,128)S(1)} fusion(s32[1536]{0:T(1024)} %copy-done.35, f32[]{:T(128)} %constant.153.clone.1, f32[16,1536]{0,1:T(8,128)} %bitcast_multiply_fusion.1), kind=kCustom, calls=%fused_computation.27 | custom fusion | flops 24576 | bytes 1114624 | tf_op jit(solution)/shard_map/scatter-add | solution.py:36
  447.8 1.8 maximum_add_fusion.1
  449.9 13.6 %fusion.81 = f32[2,16,640]{2,1,0:T(8,128)S(1)} fusion(f32[16,2,2560]{2,0,1:T(8,128)S(1)} %all_gather.61, f32[2,640,2560]{2,1,0:T(8,128)} %param.25), kind=kOutput, calls=%fused_computation.206 | convolution fusion | flops 629145600 | bytes 13516800 | tf_op jit(solution)/shard_map/tis,rts->rti/dot_general | solution.py:151
  463.8 7.4 reduce-scatter.9.cloned.1.call-done
  471.3 13.8 %multiply_reduce_fusion.4 = (f32[16]{0:T(128)S(1)}, f32[16,2,640]{2,0,1:T(8,128)S(1)}) fusion(f32[16,2,640]{2,0,1:T(8,128)S(1)} %multiply_add_fusion.2, f32[16,2,640]{2,0,1:T(8,128)} %reduce-scatter.9.cloned.1.call-done, f32[2,16,640]{2,1,0:T(8,128)S(1)} %fusion.81, f32[2,640,2560]{2,1,0:T(8,128)} %param.26, f32[16,1,2560]{2,0,1:T(8,128)S(1)} %bitcast.278, ...), kind=kOutput, calls=%fused_computation.99 | convolution fusion | flops 629309440 | bytes 13762624 | tf_op jit(solution)/shard_map/tis,rts->rti/dot_general | solution.py:154
  485.1 39.3 %psum.68 = f32[16]{0:T(128)S(1)} all-reduce(f32[16]{0:T(128)S(1)} %add.455), channel_id=1, replica_groups=mesh['day'=8,'blk'=4] {'day','blk'}, use_global_device_ids=true, to_apply=%region_31.32 | all-reduce | flops 16 | bytes 128 | tf_op jit(solution)/shard_map/psum | solution.py:174
  524.5 31.0 %all_gather.62 = f32[8,16,640]{2,1,0:T(8,128)S(1)} all-gather(f32[1,16,640]{2,1,0:T(8,128)S(1)} %fusion.43), channel_id=1, replica_groups=mesh['day'=8,'blk'=4] {'day'}, dimensions={0}, use_global_device_ids=true | all-gather | bytes 368640 | tf_op jit(solution)/shard_map/all_gather | solution.py:16
  555.5 30.9 %all-gather.2 = f32[128,640]{1,0:T(8,128)S(1)} all-gather(f32[16,640]{1,0:T(8,128)S(1)} %get-tuple-element.480), channel_id=4, replica_groups=mesh['day'=8,'blk'=4] {'day'}, dimensions={0}, use_global_device_ids=true | all-gather | bytes 368640 | tf_op jit(solution)/shard_map/all_gather | solution.py:16
  587.1 39.4 %all-reduce = (f32[16]{0:T(128)S(1)}, f32[16,64]{1,0:T(8,128)S(1)}) all-reduce(f32[16]{0:T(128)S(1)} %multiply_reduce_fusion.3, f32[16,64]{1,0:T(8,128)S(1)} %get-tuple-element.520), channel_id=1, replica_groups=mesh['day'=8,'blk'=4] {'day','blk'}, use_global_device_ids=true, to_apply=%region_38.39 | all-reduce | flops 1040 | bytes 8320 | tf_op jit(solution)/shard_map/psum | solution.py:126
  626.9 7.1 all_gather.65
  634.1 11.4 %convolution_bitcast_fusion = f32[16,2,2560]{2,0,1:T(8,128)} fusion(f32[16,2,640]{2,0,1:T(8,128)S(1)} %multiply_add_fusion.1, f32[2,640,2560]{2,1,0:T(8,128)} %param.26), kind=kOutput, calls=%fused_computation.21 | convolution fusion | flops 629145600 | bytes 13516800 | tf_op jit(solution)/shard_map/tis,rti->rts/dot_general | solution.py:155
  647.0 3.7 gather_fusion.4
  652.2 1.8 slice_bitcast_fusion
  653.9 3.9 collective-permute-start.5
  659.3 9.0 %scatter_custom_fusion.3 = f32[5120,16]{1,0:T(8,128)S(1)} fusion(s32[1536]{0:T(1024)} %copy-done.35, f32[]{:T(128)} %constant.153.clone.1, f32[16,1536]{0,1:T(8,128)} %bitcast_multiply_fusion), kind=kCustom, calls=%fused_computation.25 | custom fusion | flops 24576 | bytes 1114624 | tf_op jit(solution)/shard_map/scatter-add | solution.py:36
  671.3 1.8 maximum_add_fusion.2
  673.2 13.6 %fusion.82 = f32[2,16,640]{2,1,0:T(8,128)S(1)} fusion(f32[16,2,2560]{2,0,1:T(8,128)S(1)} %all_gather.65, f32[2,640,2560]{2,1,0:T(8,128)} %param.25), kind=kOutput, calls=%fused_computation.207 | convolution fusion | flops 629145600 | bytes 13516800 | tf_op jit(solution)/shard_map/tis,rts->rti/dot_general | solution.py:151
  687.1 7.6 %reduce-scatter.11.cloned.1.call-done = f32[16,2,640]{2,0,1:T(8,128)} async-done(((f32[16,2,2560]{2,0,1:T(8,128)}), f32[16,2,640]{2,0,1:T(8,128)}) %reduce-scatter.11.cloned.1.call-update) | async-done | bytes 81936 | tf_op jit(solution)/shard_map/reduce_scatter | solution.py:169
  694.8 13.8 %fusion.13 = f32[16]{0:T(128)S(1)} fusion(f32[16,2,640]{2,0,1:T(8,128)S(1)} %multiply_add_fusion.1, f32[16,2,640]{2,0,1:T(8,128)} %reduce-scatter.11.cloned.1.call-done, f32[2,16,640]{2,1,0:T(8,128)S(1)} %fusion.82, f32[2,640,2560]{2,1,0:T(8,128)} %param.26, f32[16,1,2560]{2,0,1:T(8,128)S(1)} %bitcast.279, f32[16,1,2560]{2,0,1:T(8,128)S(1)} %copy-done.3), kind=kOutput, calls=%fused_computation.41 | convolution fusion | flops 629309440 | bytes 13680704 | tf_op jit(solution)/shard_map/tis,rts->rti/dot_general | solution.py:154
  708.6 39.3 %psum.71 = f32[16]{0:T(128)S(1)} all-reduce(f32[16]{0:T(128)S(1)} %add.476), channel_id=1, replica_groups=mesh['day'=8,'blk'=4] {'day','blk'}, use_global_device_ids=true, to_apply=%region_46.47 | all-reduce | flops 16 | bytes 128 | tf_op jit(solution)/shard_map/psum | solution.py:174
  (235 shorter events, 39.4 us)
Async XLA Ops:
  7.2 40.2 %copy-start = (f32[64,2,256]{2,1,0:T(2,128)S(1)}, f32[64,2,256]{2,1,0:T(2,128)}, u32[]{:S(2)}) copy-start(f32[64,2,256]{2,1,0:T(2,128)} %param.33) | copy-start | bytes 393220
  7.2 112.3 %reduce-scatter.13.cloned.1.call-start = ((), (), s32[]{:S(2)}) async-start(), calls=%async_computation.7 | async-start | bytes 1638400
  10.9 27.0 %copy-start.35 = (s32[1536]{0:T(1024)}, s32[1536]{0:T(1024)S(1)}, u32[]{:S(2)}) copy-start(s32[1536]{0:T(1024)S(1)} %reshape.352) | copy-start | bytes 18436
  23.5 14.4 %copy-start.36 = (f32[2,640]{1,0:T(2,128)S(1)}, f32[2,640]{1,0:T(2,128)}, u32[]{:S(2)}) copy-start(f32[2,640]{1,0:T(2,128)} %param.27) | copy-start | bytes 15364
  37.9 208.0 %reduce-scatter.7.cloned.1.call-start = ((), (), s32[]{:S(2)}) async-start(), calls=%async_computation.4 | async-start | bytes 409600 | tf_op jit(solution)/shard_map/reduce_scatter | solution.py:169
  40.2 39.7 %copy-start.16 = (f32[15,2,640]{2,1,0:T(2,128)S(1)}, f32[15,2,640]{2,1,0:T(2,128)}, u32[]{:S(2)}) copy-start(f32[15,2,640]{2,1,0:T(2,128)} %param.36) | copy-start | bytes 230404
  47.3 144.3 %copy-start.17 = (f32[640]{0:T(1024)}, f32[640]{0:T(1024)S(1)}, u32[]{:S(2)}) copy-start(f32[640]{0:T(1024)S(1)} %get-tuple-element.405) | copy-start | bytes 7684
  47.6 144.7 %copy-start.10 = (s32[2048]{0:T(1024)}, s32[2048]{0:T(1024)S(1)}, u32[]{:S(2)}) copy-start(s32[2048]{0:T(1024)S(1)} %pad_clamp_fusion) | copy-start | bytes 24580
  80.0 130.5 %copy-start.7 = (f32[1536]{0:T(1024)}, f32[1536]{0:T(1024)S(1)}, u32[]{:S(2)}) copy-start(f32[1536]{0:T(1024)S(1)} %mul.605) | copy-start | bytes 18436
  119.4 119.6 %copy-start.29 = (f32[1,64]{1,0:T(1,128)}, f32[1,64]{1,0:T(1,128)S(1)}, u32[]{:S(2)}) copy-start(f32[1,64]{1,0:T(1,128)S(1)} %psum.64) | copy-start | bytes 772
  121.4 124.5 %copy-start.15 = (f32[1,2,640]{2,0,1:T(1,128)}, f32[1,2,640]{2,0,1:T(1,128)S(1)}, u32[]{:S(2)}) copy-start(f32[1,2,640]{2,0,1:T(1,128)S(1)} %copy.94) | copy-start | bytes 15364
  197.5 12.6 %copy-start.6 = (f32[15,64]{1,0:T(8,128)S(1)}, f32[15,64]{1,0:T(8,128)}, u32[]{:S(2)}) copy-start(f32[15,64]{1,0:T(8,128)} %param.37) | copy-start | bytes 11524
  197.5 12.6 %copy-start.20 = (f32[2,256]{1,0:T(2,128)S(1)}, f32[2,256]{1,0:T(2,128)}, u32[]{:S(2)}) copy-start(f32[2,256]{1,0:T(2,128)} %get-tuple-element.496) | copy-start | bytes 6148
  207.5 15.9 %collective-permute-start.1 = (f32[16,2560]{1,0:T(8,128)}, f32[16,2560]{1,0:T(8,128)}, u32[]{:S(2)}, u32[]{:S(2)}) collective-permute-start(f32[16,2560]{1,0:T(8,128)} %get-tuple-element.507), channel_id=1, source_target_pairs={{0,4},{4,8},{8,12},{12,16},{16,20},{20,24},{24,28},{1,5},{5,9},{9,... | collective-permute-start | bytes 491528 | tf_op jit(solution)/shard_map/ppermute | solution.py:31
  222.0 17.3 %collective-permute-start = (f32[16,2560]{1,0:T(8,128)}, f32[16,2560]{1,0:T(8,128)S(1)}, u32[]{:S(2)}, u32[]{:S(2)}) collective-permute-start(f32[16,2560]{1,0:T(8,128)} %get-tuple-element.506), channel_id=1, source_target_pairs={{4,0},{8,4},{12,8},{16,12},{20,16},{24,20},{28,24},{5,1},{9,5},{13... | collective-permute-start | bytes 491528 | tf_op jit(solution)/shard_map/ppermute | solution.py:31
  225.1 13.9 %copy-start.27 = (f32[64]{0:T(128)S(1)}, f32[64]{0:T(128)}, u32[]{:S(2)}) copy-start(f32[64]{0:T(128)} %param.35) | copy-start | bytes 772
  225.1 20.7 %copy-start.1 = (f32[16,1,2560]{2,0,1:T(8,128)S(1)}, f32[16,1,2560]{2,0,1:T(8,128)}, u32[]{:S(2)}) copy-start(f32[16,1,2560]{2,0,1:T(8,128)} %get-tuple-element.505) | copy-start | bytes 491524
  225.1 246.1 %reduce-scatter.9.cloned.1.call-start = ((), (), s32[]{:S(2)}) async-start(), calls=%async_computation.5 | async-start | bytes 409600 | tf_op jit(solution)/shard_map/reduce_scatter | solution.py:169
  245.9 84.9 %copy-start.18 = (f32[640]{0:T(1024)S(1)}, f32[640]{0:T(1024)}, u32[]{:S(2)}) copy-start(f32[640]{0:T(1024)} %copy-done.17) | copy-start | bytes 7684
  259.7 142.2 %copy-start.30 = (f32[1,64]{1,0:T(1,128)S(1)}, f32[1,64]{1,0:T(1,128)}, u32[]{:S(2)}) copy-start(f32[1,64]{1,0:T(1,128)} %copy-done.29) | copy-start | bytes 772
  299.0 111.0 %copy-start.33 = (f32[16]{0:T(128)}, f32[16]{0:T(128)S(1)}, u32[]{:S(2)}) copy-start(f32[16]{0:T(128)S(1)} %get-tuple-element.488) | copy-start | bytes 196
  402.1 26.1 %copy-start.13 = (f32[16,64]{1,0:T(8,128)}, f32[16,64]{1,0:T(8,128)S(1)}, u32[]{:S(2)}) copy-start(f32[16,64]{1,0:T(8,128)S(1)} %get-tuple-element.485) | copy-start | bytes 12292
  402.6 25.5 %copy-start.24 = (f32[16]{0:T(128)}, f32[16]{0:T(128)S(1)}, u32[]{:S(2)}) copy-start(f32[16]{0:T(128)S(1)} %get-tuple-element.482) | copy-start | bytes 196
  421.5 1.5 copy-start.11
  421.5 6.7 copy-start.31
  421.5 13.4 %copy-start.8 = (f32[1536]{0:T(1024)S(1)}, f32[1536]{0:T(1024)}, u32[]{:S(2)}) copy-start(f32[1536]{0:T(1024)} %copy-done.7) | copy-start | bytes 18436
  430.0 17.8 %collective-permute-start.3 = (f32[16,2560]{1,0:T(8,128)}, f32[16,2560]{1,0:T(8,128)}, u32[]{:S(2)}, u32[]{:S(2)}) collective-permute-start(f32[16,2560]{1,0:T(8,128)} %get-tuple-element.503), channel_id=1, source_target_pairs={{0,4},{4,8},{8,12},{12,16},{16,20},{20,24},{24,28},{1,5},{5,9},{9,... | collective-permute-start | bytes 491528 | tf_op jit(solution)/shard_map/ppermute | solution.py:31
  434.7 11.7 %copy-start.4 = (f32[16,2,256]{2,0,1:T(8,128)}, f32[16,2,256]{2,0,1:T(8,128)S(1)}, u32[]{:S(2)}) copy-start(f32[16,2,256]{2,0,1:T(8,128)S(1)} %fusion.15) | copy-start | bytes 98308
  446.5 17.4 %collective-permute-start.2 = (f32[16,2560]{1,0:T(8,128)}, f32[16,2560]{1,0:T(8,128)S(1)}, u32[]{:S(2)}, u32[]{:S(2)}) collective-permute-start(f32[16,2560]{1,0:T(8,128)} %get-tuple-element.502), channel_id=1, source_target_pairs={{4,0},{8,4},{12,8},{16,12},{20,16},{24,20},{28,24},{5,1},{9,5},{13... | collective-permute-start | bytes 491528 | tf_op jit(solution)/shard_map/ppermute | solution.py:31
  449.6 13.8 %copy-start.5 = (f32[16,2,256]{2,0,1:T(8,128)S(1)}, f32[16,2,256]{2,0,1:T(8,128)}, u32[]{:S(2)}) copy-start(f32[16,2,256]{2,0,1:T(8,128)} %copy-done.4) | copy-start | bytes 98308
  449.7 13.8 %copy-start.28 = (f32[64]{0:T(128)S(1)}, f32[64]{0:T(128)}, u32[]{:S(2)}) copy-start(f32[64]{0:T(128)} %param.35) | copy-start | bytes 772
  449.7 21.6 %copy-start.2 = (f32[16,1,2560]{2,0,1:T(8,128)S(1)}, f32[16,1,2560]{2,0,1:T(8,128)}, u32[]{:S(2)}) copy-start(f32[16,1,2560]{2,0,1:T(8,128)} %get-tuple-element.501) | copy-start | bytes 491524
  449.7 245.1 %reduce-scatter.11.cloned.1.call-start = ((), (), s32[]{:S(2)}) async-start(), calls=%async_computation.6 | async-start | bytes 409600 | tf_op jit(solution)/shard_map/reduce_scatter | solution.py:169
  471.3 53.1 %copy-start.37 = (f32[16]{0:T(128)S(1)}, f32[16]{0:T(128)}, u32[]{:S(2)}) copy-start(f32[16]{0:T(128)} %get-tuple-element.483) | copy-start | bytes 196
  471.3 84.2 %copy-start.19 = (f32[640]{0:T(1024)S(1)}, f32[640]{0:T(1024)}, u32[]{:S(2)}) copy-start(f32[640]{0:T(1024)} %copy-done.17) | copy-start | bytes 7684
  485.1 141.4 %copy-start.14 = (f32[16,64]{1,0:T(8,128)S(1)}, f32[16,64]{1,0:T(8,128)}, u32[]{:S(2)}) copy-start(f32[16,64]{1,0:T(8,128)} %copy-done.13) | copy-start | bytes 12292
  485.1 141.6 %copy-start.25 = (f32[16]{0:T(128)S(1)}, f32[16]{0:T(128)}, u32[]{:S(2)}) copy-start(f32[16]{0:T(128)} %copy-done.24) | copy-start | bytes 196
  524.4 121.1 %copy-start.22 = (f32[16]{0:T(128)}, f32[16]{0:T(128)S(1)}, u32[]{:S(2)}) copy-start(f32[16]{0:T(128)S(1)} %add_divide_fusion.1) | copy-start | bytes 196
  645.5 1.5 copy-start.12
  645.5 12.3 %copy-start.21 = (f32[2,256]{1,0:T(2,128)S(1)}, f32[2,256]{1,0:T(2,128)}, u32[]{:S(2)}) copy-start(f32[2,256]{1,0:T(2,128)} %get-tuple-element.496) | copy-start | bytes 6148
  645.5 12.6 %copy-start.9 = (f32[1536]{0:T(1024)S(1)}, f32[1536]{0:T(1024)}, u32[]{:S(2)}) copy-start(f32[1536]{0:T(1024)} %copy-done.7) | copy-start | bytes 18436
  653.9 17.4 %collective-permute-start.5 = (f32[16,2560]{1,0:T(8,128)}, f32[16,2560]{1,0:T(8,128)}, u32[]{:S(2)}, u32[]{:S(2)}) collective-permute-start(f32[16,2560]{1,0:T(8,128)} %get-tuple-element.499), channel_id=1, source_target_pairs={{0,4},{4,8},{8,12},{12,16},{16,20},{20,24},{24,28},{1,5},{5,9},{9,... | collective-permute-start | bytes 491528 | tf_op jit(solution)/shard_map/ppermute | solution.py:31
  669.8 17.4 %collective-permute-start.4 = (f32[16,2560]{1,0:T(8,128)}, f32[16,2560]{1,0:T(8,128)S(1)}, u32[]{:S(2)}, u32[]{:S(2)}) collective-permute-start(f32[16,2560]{1,0:T(8,128)} %get-tuple-element.498), channel_id=1, source_target_pairs={{4,0},{8,4},{12,8},{16,12},{20,16},{24,20},{28,24},{5,1},{9,5},{13... | collective-permute-start | bytes 491528 | tf_op jit(solution)/shard_map/ppermute | solution.py:31
  673.2 21.6 %copy-start.3 = (f32[16,1,2560]{2,0,1:T(8,128)S(1)}, f32[16,1,2560]{2,0,1:T(8,128)}, u32[]{:S(2)}) copy-start(f32[16,1,2560]{2,0,1:T(8,128)} %get-tuple-element.497) | copy-start | bytes 491524
  694.8 53.1 %copy-start.23 = (f32[16]{0:T(128)S(1)}, f32[16]{0:T(128)}, u32[]{:S(2)}) copy-start(f32[16]{0:T(128)} %copy-done.22) | copy-start | bytes 196
  694.8 53.1 %copy-start.26 = (f32[16]{0:T(128)S(1)}, f32[16]{0:T(128)}, u32[]{:S(2)}) copy-start(f32[16]{0:T(128)} %copy-done.24) | copy-start | bytes 196
  694.8 53.1 %copy-start.34 = (f32[16]{0:T(128)S(1)}, f32[16]{0:T(128)}, u32[]{:S(2)}) copy-start(f32[16]{0:T(128)} %copy-done.33) | copy-start | bytes 196
  694.8 53.3 %copy-start.32 = (f32[1,64]{1,0:T(1,128)S(1)}, f32[1,64]{1,0:T(1,128)}, u32[]{:S(2)}) copy-start(f32[1,64]{1,0:T(1,128)} %copy-done.29) | copy-start | bytes 772
Sparse Core Ops, SparseCore 0:
  38.0 29.1 reduce-scatter.12
  225.2 20.5 reduce-scatter.6
  449.8 21.4 reduce-scatter.8
  673.3 21.4 reduce-scatter.10
where the time goes:
time: 766 us; the launch traced here: 756 us
  blocking collectives  476 us (62%)
  matrix products  117 us (15%)
  other arithmetic  56.2 us (7%)
  local copies, waits for them, and re-layouts  55.5 us (7%)
  waiting for transfers between devices  21.7 us (3%)
  starting transfers between devices  15.1 us (2%)
  between operations  15 us (2%)
    all_gather x7, blocking collectives, prefix(): gathered = jax.tree.map(lambda a: lax.all_gather(a, axis), part)  218 us
    psum x3, blocking collectives, inner_norm(): lax.psum(jnp.sum(residual * preconditioned, axis=(1, 2)), ('day', 'blk'))  118 us
    psum x2, blocking collectives, on_device(): cov_total, curve_total = lax.psum((cov_terms, local_curve), ('day', 'blk'))  78.6 us
    dot_general x3, matrix products, on_device(): jnp.einsum('tis,rts->rti', off_blocks, following, precision=exact_precision)  41.4 us
    dot_general x3, matrix products, on_device(): jnp.einsum('tis,rts->rti', diag_blocks, gathered, precision=exact_precision)  40.8 us
    psum x1, blocking collectives, on_device(): lax.psum(jnp.einsum('ctj,tj->c', covariates, weighted_value, precision=ex...  39.5 us
    scatter-add x4, other arithmetic, spread(): jax.ops.segment_sum(values.reshape(leading, -1).T, flat_ids, num_segments...  35.6 us
    dot_general x3, matrix products, on_device(): jnp.einsum('tis,rti->rts', off_blocks, direction, precision=exact_precision)  32.1 us
  transfers between devices with their start and end apart: 10, of which 3 were waited for; matrix products, arithmetic and copies ran while one was open for 12% of the time, Pallas kernels for 0%

commit v1 on v0

v1 whole, which is shorter than its diff:
```python
import functools
import jax
import jax.numpy as jnp
from jax import lax
from jax.experimental import pallas as pl
from jax.experimental.pallas import tpu as pltpu
from jax.sharding import PartitionSpec as P

ITERS = 3
COLS = 256
CHUNK = 64
SLOTS = 8
MESH = pl.DeviceIdType.MESH
F32 = jnp.float32
BF16 = jnp.bfloat16


def split(x):
    hi = x.astype(BF16)
    return hi, (x - hi.astype(F32)).astype(BF16)


def nn(a, b):
    return jnp.dot(a, b, preferred_element_type=F32)


def nt(a, b, precision=None):
    return lax.dot_general(
        a, b, (((1,), (1,)), ((), ())), preferred_element_type=F32, precision=precision
    )


def kernel(
    D, B, R, dl, n, J, C,
    diag, off, vert, bary, cov, slotw, wval, leak, probes, pcov, prior,
    field_out, cov_out,
    mhi, mlo, ahi, alo, stage, stage_sem,
    dacc, own_dom, leak_all, dom_all, g_snd, g_rcv, gc_snd, gc_rcv, gcd_snd, gcd_rcv,
    x_snd, x_rcv, resid, pre, pre_rcv, npart, n_rcv, ncol, nb_rcv, pre_own, pre_full,
    dirs, dhl, ohl, part, behind, ahead, p_snd, p_rcv, q_snd, q_rcv, cc, cc_b, cs, cc_d, stepd,
    sem_blk, sem_day, sem_next,
):
    S = n * B
    T = D * dl
    Rd = R // D
    me_d = lax.axis_index("day")
    me_b = lax.axis_index("blk")

    def at_blk(k):
        return lax.rem(me_b + k, B)

    def at_day(k):
        return lax.rem(me_d + k, D)

    def start_all(copies):
        for c in copies:
            c.start()

    def wait_all(copies):
        for c in copies:
            c.wait()

    def to_blk(row, src, dst):
        return [
            pltpu.make_async_remote_copy(
                src_ref=src(at_blk(k)), dst_ref=dst(me_b),
                send_sem=sem_blk.at[0, row, k], recv_sem=sem_blk.at[1, row, k],
                device_id={"blk": at_blk(k)}, device_id_type=MESH,
            )
            for k in range(1, B)
        ]

    def to_day(row, src, dst):
        return [
            pltpu.make_async_remote_copy(
                src_ref=src(at_day(k)), dst_ref=dst(me_d),
                send_sem=sem_day.at[0, row, k], recv_sem=sem_day.at[1, row, k],
                device_id={"day": at_day(k)}, device_id_type=MESH,
            )
            for k in range(1, D)
        ]

    def to_next(row, src, dst):
        return [
            pltpu.make_async_remote_copy(
                src_ref=src(at_blk(k)), dst_ref=dst(me_b),
                send_sem=sem_next.at[0, row, k], recv_sem=sem_next.at[1, row, k],
                device_id={"day": at_day(1), "blk": at_blk(k)}, device_id_type=MESH,
            )
            for k in range(B)
        ]

    def load(mat, q, slot):
        return pltpu.make_async_copy(
            mat.at[pl.ds(pl.multiple_of(q * CHUNK, CHUNK), CHUNK)], stage.at[slot], stage_sem.at[slot]
        )

    total = dl * n // CHUNK
    per_day = n // CHUNK
    for s in range(min(SLOTS, total)):
        load(diag, s, s).start()

    barrier = pltpu.get_barrier_semaphore()
    for k in range(1, B):
        pl.semaphore_signal(barrier, inc=1, device_id={"blk": at_blk(k)}, device_id_type=MESH)
        pl.semaphore_signal(
            barrier, inc=1, device_id={"day": at_day(D - 1), "blk": at_blk(k)}, device_id_type=MESH
        )
    for k in range(1, D):
        pl.semaphore_signal(barrier, inc=1, device_id={"day": at_day(k)}, device_id_type=MESH)

    for t in range(dl):
        v = vert[t]
        b = bary[t]

        def build(c, carry):
            cols = pl.ds(pl.multiple_of(c * COLS, COLS), COLS)
            lane = lax.broadcasted_iota(jnp.int32, (J, COLS), 1) + c * COLS
            acc = jnp.zeros((J, COLS), F32)
            for k in range(3):
                acc = acc + jnp.where(v[:, k : k + 1] == lane, b[:, k : k + 1], 0.0)
            hi, lo = split(acc)
            ahi[t, :, cols] = hi
            alo[t, :, cols] = lo
            return carry

        lax.fori_loop(0, S // COLS, build, 0)

    pl.semaphore_wait(barrier, 2 * (B - 1) + D - 1)

    gc = jnp.zeros((8, C), F32)
    for t in range(dl):
        w8 = jnp.broadcast_to(wval[t], (8, J))
        gc = gc + nt(w8, cov[t], lax.Precision.HIGHEST)
        whi, wlo = split(w8)
        w2 = jnp.concatenate([whi.astype(F32), wlo.astype(F32)], axis=0).astype(BF16)

        def grad(c, carry):
            cols = pl.ds(pl.multiple_of(c * COLS, COLS), COLS)
            g = nn(w2, ahi[t, :, cols])
            part[t, 0:8, cols] = g[:8] + g[8:] + nn(w2, alo[t, :, cols])[:8]
            return carry

        lax.fori_loop(0, S // COLS, grad, 0)
        for j in range(B):
            g_snd[j, t] = part[t, 0:8, j * n : (j + 1) * n]
    gc_snd[...] = jnp.zeros_like(gc_snd)
    gc_snd[:, :C] = gc
    cc[...] = jnp.zeros_like(cc)
    first = to_blk(0, lambda j: g_snd.at[j], lambda m: g_rcv.at[m])
    first += to_blk(1, lambda j: gc_snd, lambda m: gc_rcv.at[m])
    first_leak = to_day(0, lambda g: leak, lambda m: leak_all.at[m])
    start_all(first + first_leak)
    g_rcv[me_b] = g_snd[me_b]
    gc_rcv[me_b] = gc_snd[...]
    leak_all[me_d] = leak[...]

    def convert(mat, base, want_diagonal):
        def one(q, carry):
            slot = lax.rem(q, SLOTS)
            load(mat, q, slot).wait()
            x = stage[slot]
            hi, lo = split(x)
            rows = pl.ds(pl.multiple_of(base + q * CHUNK, CHUNK), CHUNK)
            mhi[rows] = hi
            mlo[rows] = lo
            if want_diagonal:
                first_row = me_b * n + lax.rem(q, per_day) * CHUNK
                gap = lax.broadcasted_iota(jnp.int32, (CHUNK, S), 1) - lax.broadcasted_iota(
                    jnp.int32, (CHUNK, S), 0
                )
                picked = jnp.where(gap == first_row, x, 0.0)
                t = q // per_day
                dacc[t] = dacc[t] + jnp.sum(picked.reshape(CHUNK // 8, 8, S), axis=0)

            @pl.when(q + SLOTS < total)
            def _():
                load(mat, q + SLOTS, slot).start()

            return carry

        lax.fori_loop(0, total, one, 0)

    dacc[...] = jnp.zeros_like(dacc)
    convert(diag, 0, True)
    for s in range(min(SLOTS, total)):
        load(off, s, s).start()
    for t in range(dl):
        row = jnp.sum(dacc[t], axis=0, keepdims=True)
        acc = row[:, :n]
        for j in range(1, B):
            acc = acc + row[:, j * n : (j + 1) * n]
        own_dom[t : t + 1] = acc
    first_dom = to_day(1, lambda g: own_dom, lambda m: dom_all.at[m])
    start_all(first_dom)
    dom_all[me_d] = own_dom[...]

    wait_all(first)
    g_own = jnp.sum(g_rcv[...], axis=0)
    gcd_snd[...] = jnp.sum(gc_rcv[...], axis=0)
    is_first = lax.broadcasted_iota(jnp.int32, (R, 1), 0) == 0
    for t in range(dl):
        r = jnp.where(is_first, jnp.broadcast_to(g_own[t, 0:1], (R, n)), probes[t])
        for g in range(D):
            x_snd[g, t] = r[g * Rd : (g + 1) * Rd]
    move = to_day(2, lambda g: x_snd.at[g], lambda m: x_rcv.at[0, m])
    move += to_day(3, lambda g: gcd_snd, lambda m: gcd_rcv.at[m])
    start_all(move)
    x_rcv[0, me_d] = x_snd[me_d]
    gcd_rcv[me_d] = gcd_snd[...]
    convert(off, dl * n, False)
    wait_all(first_leak + first_dom + move)
    gcov = jnp.sum(gcd_rcv[...], axis=0)[0:1, :C]
    resid_cov = jnp.where(is_first, jnp.broadcast_to(gcov, (R, C)), pcov[...])
    resid[...] = x_rcv[0]
    pre[T] = jnp.zeros((Rd, n), F32)

    live = jnp.where(me_d == D - 1, 0.0, 1.0).astype(F32)
    norm_now = None
    sol_cov = jnp.zeros((R, C), F32)
    dir_cov = None
    row_day = 4
    row_blk = 2
    for it in range(ITERS):
        running = jnp.zeros((Rd, n), F32)
        for t in range(T):
            decay = 1.0 - leak_all[t // dl, t % dl : t % dl + 1]
            running = resid[t // dl, t % dl] + decay * running
            pre[t] = running / dom_all[t // dl, t % dl : t % dl + 1]
        running = pre[T - 1]
        norm_part = resid[D - 1, dl - 1] * running
        for t in range(T - 2, -1, -1):
            u = t + 1
            decay = 1.0 - leak_all[u // dl, u % dl : u % dl + 1]
            running = pre[t] + decay * running
            pre[t] = running
            norm_part = norm_part + resid[t // dl, t % dl] * running
        npart[...] = jnp.broadcast_to(jnp.sum(norm_part, axis=1, keepdims=True), (Rd, 128))
        back = to_day(
            row_day, lambda g: pre.at[pl.ds(g * dl, dl + 1)], lambda m: pre_rcv.at[it, m]
        )
        back += to_day(row_day + 1, lambda g: npart, lambda m: n_rcv.at[it, m])
        start_all(back)
        for t in range(dl + 1):
            pre_rcv[it, me_d, t] = pre[me_d * dl + t]
        n_rcv[it, me_d] = npart[...]
        wait_all(back)
        for g in range(D):
            for t in range(dl + 1):
                pre_own[t, g * Rd : (g + 1) * Rd] = pre_rcv[it, g, t]
            ncol[g * Rd : (g + 1) * Rd] = n_rcv[it, g]
        spread_out = to_blk(row_blk, lambda j: pre_own, lambda m: pre_full.at[it, m])
        spread_out += to_blk(row_blk + 1, lambda j: ncol, lambda m: nb_rcv.at[it, m])
        start_all(spread_out)
        pre_full[it, me_b] = pre_own[...]
        nb_rcv[it, me_b] = ncol[...]
        wait_all(spread_out)
        norm_next = jnp.sum(nb_rcv[it], axis=0)[:, 0:1] + jnp.sum(
            resid_cov * resid_cov, axis=1, keepdims=True
        )
        if it == 0:
            dir_cov = resid_cov
        else:
            beta = norm_next / norm_now
            dir_cov = resid_cov + beta * dir_cov
        norm_now = norm_next
        for j in range(B):
            for t in range(dl + 1):
                d = pre_full[it, j, t]
                if it > 0:
                    d = d + beta * dirs[it - 1, j, t]
                dirs[it, j, t] = d
                hi, lo = split(d)
                dhl[t, 0:R, j * n : (j + 1) * n] = hi
                dhl[t, R : 2 * R, j * n : (j + 1) * n] = lo
        for t in range(dl):
            d = dirs[it, me_b, t]
            hi, lo = split(d)
            ohl[t, 0:R] = hi
            ohl[t, R : 2 * R] = lo

        curve = jnp.zeros((R, 1), F32)
        cov_terms = jnp.zeros((R, C), F32)
        for t in range(dl):
            both = nt(dhl[t], ahi[t])
            predictor = both[:R] + both[R:] + nt(dhl[t, 0:R], alo[t])
            predictor = predictor + jnp.dot(
                dir_cov, cov[t], preferred_element_type=F32, precision=lax.Precision.HIGHEST
            )
            weighted = slotw[t] * predictor
            cov_terms = cov_terms + nt(weighted, cov[t], lax.Precision.HIGHEST)
            whi, wlo = split(weighted)
            w2 = jnp.concatenate([whi, wlo], axis=0)

            def columns(c, carry):
                cols = pl.ds(pl.multiple_of(c * COLS, COLS), COLS)
                rows = slice(t * n, (t + 1) * n)
                orows = slice((dl + t) * n, (dl + t + 1) * n)
                dv = ohl[t]
                x = nn(dv, mhi[rows, cols]) + nn(w2, ahi[t, :, cols])
                y = nn(dv[:R], mlo[rows, cols]) + nn(whi, alo[t, :, cols])
                part[t, :, cols] = x[:R] + x[R:] + y
                x = nn(dv, mhi[orows, cols])
                behind[t, :, cols] = x[:R] + x[R:] + nn(dv[:R], mlo[orows, cols])
                return carry

            lax.fori_loop(0, S // COLS, columns, 0)
            x = nt(dhl[t + 1], mhi[(dl + t) * n : (dl + t + 1) * n])
            ahead[t] = x[:R] + x[R:] + nt(dhl[t + 1, 0:R], mlo[(dl + t) * n : (dl + t + 1) * n])
            curve = curve + jnp.sum(ahead[t] * dirs[it, me_b, t], axis=1, keepdims=True)
        for j in range(B):
            piece = slice(j * n, (j + 1) * n)
            for t in range(dl):
                p = part[t, :, piece]
                if t > 0:
                    p = p + behind[t - 1, :, piece]
                p_snd[j, t] = p
                curve = curve + jnp.sum(p * dirs[it, j, t], axis=1, keepdims=True)
            q = behind[dl - 1, :, piece] * live
            q_snd[j] = q
            curve = curve + jnp.sum(q * dirs[it, j, dl], axis=1, keepdims=True)
        curve = curve + jnp.sum(dir_cov * cov_terms, axis=1, keepdims=True)
        cc[0, :, :C] = cov_terms
        cc[1] = jnp.broadcast_to(curve, (R, 128))
        last = it + 1 == ITERS
        reduce = to_blk(row_blk + 2, lambda j: cc, lambda m: cc_b.at[it, m])
        if not last:
            reduce += to_blk(row_blk + 3, lambda j: p_snd.at[j], lambda m: p_rcv.at[it, m])
            reduce += to_next(it, lambda j: q_snd.at[j], lambda m: q_rcv.at[it, m])
        start_all(reduce)
        cc_b[it, me_b] = cc[...]
        if not last:
            p_rcv[it, me_b] = p_snd[me_b]
        wait_all(reduce)
        cs[...] = jnp.sum(cc_b[it], axis=0)
        share = to_day(row_day + 2, lambda g: cs, lambda m: cc_d.at[it, m])
        if not last:
            for t in range(dl):
                image = jnp.sum(p_rcv[it, :, t], axis=0) + ahead[t]
                if t == 0:
                    image = image + jnp.sum(q_rcv[it], axis=0)
                for g in range(D):
                    x_snd[g, t] = image[g * Rd : (g + 1) * Rd]
            share += to_day(row_day + 3, lambda g: x_snd.at[g], lambda m: x_rcv.at[it + 1, m])
        start_all(share)
        cc_d[it, me_d] = cs[...]
        if not last:
            x_rcv[it + 1, me_d] = x_snd[me_d]
        wait_all(share)
        summed = jnp.sum(cc_d[it], axis=0)
        prior_dir = prior[...] * dir_cov
        image_cov = summed[0, :, :C] + prior_dir
        curvature = summed[1, :, 0:1] + jnp.sum(dir_cov * prior_dir, axis=1, keepdims=True)
        step = norm_now / curvature
        for t in range(dl):
            add = step * dirs[it, me_b, t]
            field_out[t] = add if it == 0 else field_out[t] + add
        sol_cov = sol_cov + step * dir_cov
        if not last:
            resid_cov = resid_cov - step * image_cov
            wide = jnp.broadcast_to(step, (R, 128))
            for g in range(D):
                stepd[g] = wide[g * Rd : (g + 1) * Rd]
            own_step = stepd[me_d][:, 0:1]
            for g in range(D):
                for t in range(dl):
                    resid[g, t] = resid[g, t] - own_step * x_rcv[it + 1, g, t]
        row_day += 4
        row_blk += 4
    cov_out[...] = sol_cov


def on_device(
    D, B,
    diag_blocks, off_blocks, leakage, obs_count, obs_triangle, obs_bary, obs_prec, obs_value,
    covariates, triangles, prior_prec, probes, probes_cov,
):
    dl, n, S = diag_blocks.shape
    J = obs_triangle.shape[1]
    C = covariates.shape[0]
    R = probes.shape[0] + 1
    Rd = R // D
    slot_index = lax.broadcasted_iota(jnp.int32, obs_triangle.shape, 1) + lax.axis_index("blk") * J
    slot_weight = jnp.where(slot_index < obs_count[:, None], obs_prec, jnp.zeros_like(obs_prec))
    vert = jnp.moveaxis(triangles[:, obs_triangle], 0, 2)
    bary = jnp.moveaxis(obs_bary / jnp.sum(obs_bary, axis=0, keepdims=True), 0, 2)
    cov = jnp.moveaxis(covariates, 0, 1)
    padded = jnp.moveaxis(jnp.concatenate([jnp.zeros_like(probes[:1]), probes], axis=0), 0, 1)
    pcov = jnp.concatenate([jnp.zeros_like(probes_cov[:1]), probes_cov], axis=0)
    vm = pltpu.VMEM
    rows = 2 * dl * n
    rows_blk = 2 + 4 * ITERS
    rows_day = 4 + 4 * ITERS
    scratch = [
        vm((rows, S), BF16), vm((rows, S), BF16), vm((dl, J, S), BF16), vm((dl, J, S), BF16),
        vm((SLOTS, CHUNK, S), F32), pltpu.SemaphoreType.DMA((SLOTS,)),
        vm((dl, 8, S), F32), vm((dl, n), F32), vm((D, dl, n), F32), vm((D, dl, n), F32),
        vm((B, dl, 8, n), F32), vm((B, dl, 8, n), F32), vm((8, 128), F32), vm((B, 8, 128), F32),
        vm((8, 128), F32), vm((D, 8, 128), F32),
        vm((D, dl, Rd, n), F32), vm((ITERS, D, dl, Rd, n), F32), vm((D, dl, Rd, n), F32),
        vm((D * dl + 1, Rd, n), F32), vm((ITERS, D, dl + 1, Rd, n), F32),
        vm((Rd, 128), F32), vm((ITERS, D, Rd, 128), F32), vm((R, 128), F32),
        vm((ITERS, B, R, 128), F32), vm((dl + 1, R, n), F32), vm((ITERS, B, dl + 1, R, n), F32),
        vm((ITERS, B, dl + 1, R, n), F32), vm((dl + 1, 2 * R, S), BF16), vm((dl, 2 * R, n), BF16),
        vm((dl, R, S), F32), vm((dl, R, S), F32), vm((dl, R, n), F32),
        vm((B, dl, R, n), F32), vm((ITERS - 1, B, dl, R, n), F32),
        vm((B, R, n), F32), vm((ITERS - 1, B, R, n), F32),
        vm((2, R, 128), F32), vm((ITERS, B, 2, R, 128), F32), vm((2, R, 128), F32),
        vm((ITERS, D, 2, R, 128), F32), vm((D, Rd, 128), F32),
        pltpu.SemaphoreType.DMA((2, rows_blk, B)), pltpu.SemaphoreType.DMA((2, rows_day, D)),
        pltpu.SemaphoreType.DMA((2, ITERS - 1, B)),
    ]
    anywhere = pl.BlockSpec(memory_space=pltpu.HBM)
    inside = pl.BlockSpec(memory_space=pltpu.VMEM)
    field, out_cov = pl.pallas_call(
        functools.partial(kernel, D, B, R, dl, n, J, C),
        out_shape=(jax.ShapeDtypeStruct((dl, R, n), F32), jax.ShapeDtypeStruct((R, C), F32)),
        in_specs=[anywhere] * 2 + [inside] * 9,
        out_specs=(inside, inside),
        scratch_shapes=scratch,
        compiler_params=pltpu.CompilerParams(
            collective_id=0, has_side_effects=True, vmem_limit_bytes=60 * 1024 * 1024
        ),
    )(
        diag_blocks.reshape(dl * n, S), off_blocks.reshape(dl * n, S), vert, bary, cov,
        slot_weight[:, None], (slot_weight * obs_value)[:, None], leakage, padded, pcov,
        prior_prec[None],
    )
    return (jnp.moveaxis(field, 0, 1), out_cov)


def solution(mesh):
    in_specs = (
        P("day", "blk", None),
        P("day", "blk", None),
        P("day", "blk"),
        P("day"),
        P("day", "blk"),
        P(None, "day", "blk"),
        P("day", "blk"),
        P("day", "blk"),
        P(None, "day", "blk"),
        P(),
        P(),
        P(None, "day", "blk"),
        P(),
    )
    out_specs = (P(None, "day", "blk"), P())
    body = functools.partial(on_device, mesh.shape["day"], mesh.shape["blk"])
    return jax.shard_map(
        body, mesh=mesh, in_specs=in_specs, out_specs=out_specs, check_vma=False
    )
```

time: 766 us -> 158 us (0.21); the launches traced: 756 us -> 158 us
  blocking collectives: 476 us -> 0 us
  Pallas kernels: 0 us -> 141 us
  matrix products: 117 us -> 0 us
  other arithmetic: 56.2 us -> 2.87 us
  local copies, waits for them, and re-layouts: 55.5 us -> 12.6 us
  waiting for transfers between devices: 21.7 us -> 0 us
  starting transfers between devices: 15.1 us -> 0 us
  between operations: 15 us -> 0.65 us
    all_gather x10 -> x0, blocking collectives: 239 us -> none  [the longest x7 218 us: prefix(): gathered = jax.tree.map(lambda a: lax.all_gather(a, axis), part)]
    psum x6 -> x0, blocking collectives: 236 us -> none  [the longest x3 118 us: inner_norm(): lax.psum(jnp.sum(residual * preconditioned, axis=(1, 2)), ('day', 'blk'))]
    pallas_call x0 -> x1, Pallas kernels: none -> 141 us  [on_device(): pl.pallas_call(functools.partial(kernel, D, B, R, dl, n, J, C), out_shape...]
    dot_general x16 -> x0, matrix products: 117 us -> none  [the longest x3 41.4 us: on_device(): jnp.einsum('tis,rts->rti', off_blocks, following, precision=exact_precision)]
    scatter-add x4 -> x0, other arithmetic: 35.6 us -> none  [spread(): jax.ops.segment_sum(values.reshape(leading, -1).T, flat_ids, num_segments...]
    reduce_scatter x3 -> x0, waiting for transfers between devices: 21.6 us -> none  [on_device(): lax.psum_scatter(obs_terms + earlier, 'blk', scatter_dimension=2, tiled=T...]
    unnamed x86 -> x6, local copies, waits for them, and re-layouts: 22.6 us -> 6.97 us
    gather x6 -> x1, local copies, waits for them, and re-layouts: 16.7 us -> 1.64 us  [on_device(): vert = jnp.moveaxis(triangles[:, obs_triangle], 0, 2)]
  transfers between devices with their start and end apart: 10 -> 0, of which waited for: 3 -> 0; matrix products, arithmetic and copies ran while one was open for 12% -> 0% of each run, Pallas kernels for 0% -> 0%
where the time goes in v1:
time: 158 us
  Pallas kernels  141 us (89%)
  local copies, waits for them, and re-layouts  12.6 us (8%)
  other arithmetic  2.87 us (2%)
    pallas_call x1, Pallas kernels, on_device(): pl.pallas_call(functools.partial(kernel, D, B, R, dl, n, J, C), out_shape...  141 us
    unnamed x6, local copies, waits for them, and re-layouts  6.97 us

profile of v1, /device:TPU:0, one launch (start us, length us, event | category | flops | bytes accessed | tf_op | source)
XLA Modules:
  0.0 157.5 jit_solution(2997054144304183980)
XLA Ops:
  0.6 1.7 %copy.15 = s32[3,5116]{0,1:T(8,128)S(1)} copy(s32[3,5116]{1,0:T(4,128)} %param.22) | data formatting | bytes 122784 | tf_op args[9]
  2.3 0.7 fusion
  3.0 1.6 %gather_fusion = s32[512,3]{1,0:T(8,128)} fusion(s32[3,5116]{0,1:T(8,128)S(1)} %copy.15, s32[1024]{0:T(1024)S(1)} %pad_clamp_fusion), kind=kCustom, calls=%fused_computation | custom fusion | bytes 14336 | tf_op jit(solution)/shard_map/gather | solution.py:385
  4.6 0.7 reduce_sum.9
  5.3 0.7 broadcast_divide_fusion
  6.0 0.9 copy.17
  6.9 1.6 copy.25
  8.5 0.8 fusion.1
  9.2 0.6 copy.20.slotw
  9.8 0.6 broadcast_in_dim.22.wval
  10.4 0.9 copy.19
  11.3 0.6 pad_bitcast_fusion.probes
  11.9 1.3 concatenate.7.pcov
  13.2 141.4 %shard_map.140 = (f32[2,16,640]{2,1,0:T(8,128)}, f32[16,64]{1,0:T(8,128)}) custom-call(f32[1280,2560]{1,0:T(8,128)} %bitcast.16, f32[1280,2560]{1,0:T(8,128)} %bitcast.17, s32[2,256,3]{2,1,0:T(8,128)} %bitcast.20, f32[2,256,3]{2,1,0:T(8,128)} %bitcast.18, f32[2,64,256]{2,1,0:T(8,128)} %bitcast.19, f32[2,1,256]{2,1,0:T(1,128)} %copy.20.slotw, ...), custom_call_target="tpu_custom_call" | custom-call | tf_op jit(solution)/shard_map/pallas_call | solution.py:415
  154.7 1.6 copy.21
  156.2 1.3 copy.27
  (3 shorter events, 0.0 us)

commit v2 on v1

--- a/solution.py
+++ b/solution.py
@@ -32,11 +32,11 @@
 
 def kernel(
     D, B, R, dl, n, J, C,
-    diag, off, vert, bary, cov, slotw, wval, leak, probes, pcov, prior,
+    diag, off, vert, bary, cov_in, slotw, value, leak, probes, pcov, prior,
     field_out, cov_out,
     mhi, mlo, ahi, alo, stage, stage_sem,
     dacc, own_dom, leak_all, dom_all, g_snd, g_rcv, gc_snd, gc_rcv, gcd_snd, gcd_rcv,
-    x_snd, x_rcv, resid, pre, pre_rcv, npart, n_rcv, ncol, nb_rcv, pre_own, pre_full,
+    cov, rawd, rawb, x_snd, x_rcv, resid, pre, pre_rcv, npart, n_rcv, ncol, nb_rcv, pre_own, pre_full,
     dirs, dhl, ohl, part, behind, ahead, p_snd, p_rcv, q_snd, q_rcv, cc, cc_b, cs, cc_d, stepd,
     sem_blk, sem_day, sem_next,
 ):
@@ -110,18 +110,21 @@
         pl.semaphore_signal(barrier, inc=1, device_id={"day": at_day(k)}, device_id_type=MESH)
 
     for t in range(dl):
-        v = vert[t]
-        b = bary[t]
+        cov[t] = cov_in[:, t, :]
+        corner = [vert[k, t : t + 1, :] for k in range(3)]
+        raw = [bary[k, t : t + 1, :] for k in range(3)]
+        scale = raw[0] + raw[1] + raw[2]
+        share_of = [x / scale for x in raw]
 
         def build(c, carry):
-            cols = pl.ds(pl.multiple_of(c * COLS, COLS), COLS)
-            lane = lax.broadcasted_iota(jnp.int32, (J, COLS), 1) + c * COLS
-            acc = jnp.zeros((J, COLS), F32)
+            nodes = pl.ds(pl.multiple_of(c * COLS, COLS), COLS)
+            node = lax.broadcasted_iota(jnp.int32, (COLS, J), 0) + c * COLS
+            acc = jnp.zeros((COLS, J), F32)
             for k in range(3):
-                acc = acc + jnp.where(v[:, k : k + 1] == lane, b[:, k : k + 1], 0.0)
+                acc = acc + jnp.where(corner[k] == node, share_of[k], 0.0)
             hi, lo = split(acc)
-            ahi[t, :, cols] = hi
-            alo[t, :, cols] = lo
+            ahi[t, nodes] = hi
+            alo[t, nodes] = lo
             return carry
 
         lax.fori_loop(0, S // COLS, build, 0)
@@ -130,15 +133,15 @@
 
     gc = jnp.zeros((8, C), F32)
     for t in range(dl):
-        w8 = jnp.broadcast_to(wval[t], (8, J))
+        w8 = jnp.broadcast_to(slotw[t : t + 1] * value[t : t + 1], (8, J))
         gc = gc + nt(w8, cov[t], lax.Precision.HIGHEST)
         whi, wlo = split(w8)
         w2 = jnp.concatenate([whi.astype(F32), wlo.astype(F32)], axis=0).astype(BF16)
 
         def grad(c, carry):
             cols = pl.ds(pl.multiple_of(c * COLS, COLS), COLS)
-            g = nn(w2, ahi[t, :, cols])
-            part[t, 0:8, cols] = g[:8] + g[8:] + nn(w2, alo[t, :, cols])[:8]
+            g = nt(w2, ahi[t, cols])
+            part[t, 0:8, cols] = g[:8] + g[8:] + nt(w2, alo[t, cols])[:8]
             return carry
 
         lax.fori_loop(0, S // COLS, grad, 0)
@@ -198,9 +201,10 @@
     wait_all(first)
     g_own = jnp.sum(g_rcv[...], axis=0)
     gcd_snd[...] = jnp.sum(gc_rcv[...], axis=0)
-    is_first = lax.broadcasted_iota(jnp.int32, (R, 1), 0) == 0
     for t in range(dl):
-        r = jnp.where(is_first, jnp.broadcast_to(g_own[t, 0:1], (R, n)), probes[t])
+        pre_own[t, 0:1] = g_own[t, 0:1]
+        pre_own[t, 1:R] = probes[:, t, :]
+        r = pre_own[t]
         for g in range(D):
             x_snd[g, t] = r[g * Rd : (g + 1) * Rd]
     move = to_day(2, lambda g: x_snd.at[g], lambda m: x_rcv.at[0, m])
@@ -210,8 +214,9 @@
     gcd_rcv[me_d] = gcd_snd[...]
     convert(off, dl * n, False)
     wait_all(first_leak + first_dom + move)
-    gcov = jnp.sum(gcd_rcv[...], axis=0)[0:1, :C]
-    resid_cov = jnp.where(is_first, jnp.broadcast_to(gcov, (R, C)), pcov[...])
+    ncol[0:1] = jnp.sum(gcd_rcv[...], axis=0)[0:1]
+    ncol[1:R, 0:C] = pcov[...]
+    resid_cov = ncol[:, 0:C]
     resid[...] = x_rcv[0]
     pre[T] = jnp.zeros((Rd, n), F32)
 
@@ -249,21 +254,52 @@
             for t in range(dl + 1):
                 pre_own[t, g * Rd : (g + 1) * Rd] = pre_rcv[it, g, t]
             ncol[g * Rd : (g + 1) * Rd] = n_rcv[it, g]
+        norms = to_blk(row_blk + 1, lambda j: ncol, lambda m: nb_rcv.at[it, m])
         spread_out = to_blk(row_blk, lambda j: pre_own, lambda m: pre_full.at[it, m])
-        spread_out += to_blk(row_blk + 1, lambda j: ncol, lambda m: nb_rcv.at[it, m])
-        start_all(spread_out)
+        start_all(norms + spread_out)
         pre_full[it, me_b] = pre_own[...]
         nb_rcv[it, me_b] = ncol[...]
-        wait_all(spread_out)
+        last = it + 1 == ITERS
+
+        for t in range(dl):
+            hi, lo = split(pre_own[t])
+            ohl[t, 0:R] = hi
+            ohl[t, R : 2 * R] = lo
+
+            def columns(c, carry):
+                cols = pl.ds(pl.multiple_of(c * COLS, COLS), COLS)
+                rows = slice(t * n, (t + 1) * n)
+                orows = slice((dl + t) * n, (dl + t + 1) * n)
+                dv = ohl[t]
+                x = nn(dv, mhi[rows, cols])
+                rawd[t, :, cols] = x[:R] + x[R:] + nn(dv[:R], mlo[rows, cols])
+                x = nn(dv, mhi[orows, cols])
+                rawb[t, :, cols] = x[:R] + x[R:] + nn(dv[:R], mlo[orows, cols])
+                return carry
+
+            lax.fori_loop(0, S // COLS, columns, 0)
+        wait_all(norms)
         norm_next = jnp.sum(nb_rcv[it], axis=0)[:, 0:1] + jnp.sum(
             resid_cov * resid_cov, axis=1, keepdims=True
         )
         if it == 0:
             dir_cov = resid_cov
+            part[...] = rawd[...]
+            behind[...] = rawb[...]
         else:
             beta = norm_next / norm_now
             dir_cov = resid_cov + beta * dir_cov
+            for t in range(dl):
+                part[t] = rawd[t] + beta * part[t]
+                behind[t] = rawb[t] + beta * behind[t]
         norm_now = norm_next
+        ahead_send = []
+        if not last:
+            for j in range(B):
+                q_snd[j] = behind[dl - 1, :, j * n : (j + 1) * n] * live
+            ahead_send = to_next(it, lambda j: q_snd.at[j], lambda m: q_rcv.at[it, m])
+            start_all(ahead_send)
+        wait_all(spread_out)
         for j in range(B):
             for t in range(dl + 1):
                 d = pre_full[it, j, t]
@@ -273,65 +309,58 @@
                 hi, lo = split(d)
                 dhl[t, 0:R, j * n : (j + 1) * n] = hi
                 dhl[t, R : 2 * R, j * n : (j + 1) * n] = lo
-        for t in range(dl):
-            d = dirs[it, me_b, t]
-            hi, lo = split(d)
-            ohl[t, 0:R] = hi
-            ohl[t, R : 2 * R] = lo
 
         curve = jnp.zeros((R, 1), F32)
         cov_terms = jnp.zeros((R, C), F32)
         for t in range(dl):
-            both = nt(dhl[t], ahi[t])
-            predictor = both[:R] + both[R:] + nt(dhl[t, 0:R], alo[t])
+            both = nn(dhl[t], ahi[t])
+            predictor = both[:R] + both[R:] + nn(dhl[t, 0:R], alo[t])
             predictor = predictor + jnp.dot(
                 dir_cov, cov[t], preferred_element_type=F32, precision=lax.Precision.HIGHEST
             )
-            weighted = slotw[t] * predictor
-            cov_terms = cov_terms + nt(weighted, cov[t], lax.Precision.HIGHEST)
-            whi, wlo = split(weighted)
-            w2 = jnp.concatenate([whi, wlo], axis=0)
-
-            def columns(c, carry):
-                cols = pl.ds(pl.multiple_of(c * COLS, COLS), COLS)
-                rows = slice(t * n, (t + 1) * n)
-                orows = slice((dl + t) * n, (dl + t + 1) * n)
-                dv = ohl[t]
-                x = nn(dv, mhi[rows, cols]) + nn(w2, ahi[t, :, cols])
-                y = nn(dv[:R], mlo[rows, cols]) + nn(whi, alo[t, :, cols])
-                part[t, :, cols] = x[:R] + x[R:] + y
-                x = nn(dv, mhi[orows, cols])
-                behind[t, :, cols] = x[:R] + x[R:] + nn(dv[:R], mlo[orows, cols])
-                return carry
-
-            lax.fori_loop(0, S // COLS, columns, 0)
-            x = nt(dhl[t + 1], mhi[(dl + t) * n : (dl + t + 1) * n])
-            ahead[t] = x[:R] + x[R:] + nt(dhl[t + 1, 0:R], mlo[(dl + t) * n : (dl + t + 1) * n])
-            curve = curve + jnp.sum(ahead[t] * dirs[it, me_b, t], axis=1, keepdims=True)
+            weighted = slotw[t : t + 1] * predictor
+            curve = curve + jnp.sum(weighted * predictor, axis=1, keepdims=True)
+            if not last:
+                cov_terms = cov_terms + nt(weighted, cov[t], lax.Precision.HIGHEST)
+                whi, wlo = split(weighted)
+                w2 = jnp.concatenate([whi, wlo], axis=0)
+
+                def observed(c, carry):
+                    cols = pl.ds(pl.multiple_of(c * COLS, COLS), COLS)
+                    x = nt(w2, ahi[t, cols])
+                    rawd[t, :, cols] = x[:R] + x[R:] + nt(whi, alo[t, cols])
+                    return carry
+
+                lax.fori_loop(0, S // COLS, observed, 0)
+        acc = [jnp.zeros((R, n), F32) for _ in range(2)]
         for j in range(B):
             piece = slice(j * n, (j + 1) * n)
             for t in range(dl):
                 p = part[t, :, piece]
-                if t > 0:
-                    p = p + behind[t - 1, :, piece]
-                p_snd[j, t] = p
-                curve = curve + jnp.sum(p * dirs[it, j, t], axis=1, keepdims=True)
-            q = behind[dl - 1, :, piece] * live
-            q_snd[j] = q
-            curve = curve + jnp.sum(q * dirs[it, j, dl], axis=1, keepdims=True)
-        curve = curve + jnp.sum(dir_cov * cov_terms, axis=1, keepdims=True)
+                q = behind[t, :, piece]
+                acc[0] = acc[0] + p * dirs[it, j, t]
+                acc[1] = acc[1] + q * dirs[it, j, t + 1]
+                if not last:
+                    p = p + rawd[t, :, piece]
+                    if t > 0:
+                        p = p + behind[t - 1, :, piece]
+                    p_snd[j, t] = p
+        curve = curve + jnp.sum(acc[0] + 2.0 * acc[1], axis=1, keepdims=True)
         cc[0, :, :C] = cov_terms
         cc[1] = jnp.broadcast_to(curve, (R, 128))
-        last = it + 1 == ITERS
         reduce = to_blk(row_blk + 2, lambda j: cc, lambda m: cc_b.at[it, m])
         if not last:
             reduce += to_blk(row_blk + 3, lambda j: p_snd.at[j], lambda m: p_rcv.at[it, m])
-            reduce += to_next(it, lambda j: q_snd.at[j], lambda m: q_rcv.at[it, m])
         start_all(reduce)
         cc_b[it, me_b] = cc[...]
         if not last:
             p_rcv[it, me_b] = p_snd[me_b]
-        wait_all(reduce)
+            for t in range(dl):
+                x = nt(dhl[t + 1], mhi[(dl + t) * n : (dl + t + 1) * n])
+                ahead[t] = (
+                    x[:R] + x[R:] + nt(dhl[t + 1, 0:R], mlo[(dl + t) * n : (dl + t + 1) * n])
+                )
+        wait_all(reduce + ahead_send)
         cs[...] = jnp.sum(cc_b[it], axis=0)
         share = to_day(row_day + 2, lambda g: cs, lambda m: cc_d.at[it, m])
         if not last:
@@ -382,21 +411,18 @@
     Rd = R // D
     slot_index = lax.broadcasted_iota(jnp.int32, obs_triangle.shape, 1) + lax.axis_index("blk") * J
     slot_weight = jnp.where(slot_index < obs_count[:, None], obs_prec, jnp.zeros_like(obs_prec))
-    vert = jnp.moveaxis(triangles[:, obs_triangle], 0, 2)
-    bary = jnp.moveaxis(obs_bary / jnp.sum(obs_bary, axis=0, keepdims=True), 0, 2)
-    cov = jnp.moveaxis(covariates, 0, 1)
-    padded = jnp.moveaxis(jnp.concatenate([jnp.zeros_like(probes[:1]), probes], axis=0), 0, 1)
-    pcov = jnp.concatenate([jnp.zeros_like(probes_cov[:1]), probes_cov], axis=0)
+    vert = triangles[:, obs_triangle]
     vm = pltpu.VMEM
     rows = 2 * dl * n
     rows_blk = 2 + 4 * ITERS
     rows_day = 4 + 4 * ITERS
     scratch = [
-        vm((rows, S), BF16), vm((rows, S), BF16), vm((dl, J, S), BF16), vm((dl, J, S), BF16),
+        vm((rows, S), BF16), vm((rows, S), BF16), vm((dl, S, J), BF16), vm((dl, S, J), BF16),
         vm((SLOTS, CHUNK, S), F32), pltpu.SemaphoreType.DMA((SLOTS,)),
         vm((dl, 8, S), F32), vm((dl, n), F32), vm((D, dl, n), F32), vm((D, dl, n), F32),
         vm((B, dl, 8, n), F32), vm((B, dl, 8, n), F32), vm((8, 128), F32), vm((B, 8, 128), F32),
         vm((8, 128), F32), vm((D, 8, 128), F32),
+        vm((dl, C, J), F32), vm((dl, R, S), F32), vm((dl, R, S), F32),
         vm((D, dl, Rd, n), F32), vm((ITERS, D, dl, Rd, n), F32), vm((D, dl, Rd, n), F32),
         vm((D * dl + 1, Rd, n), F32), vm((ITERS, D, dl + 1, Rd, n), F32),
         vm((Rd, 128), F32), vm((ITERS, D, Rd, 128), F32), vm((R, 128), F32),
@@ -422,9 +448,8 @@
             collective_id=0, has_side_effects=True, vmem_limit_bytes=60 * 1024 * 1024
         ),
     )(
-        diag_blocks.reshape(dl * n, S), off_blocks.reshape(dl * n, S), vert, bary, cov,
-        slot_weight[:, None], (slot_weight * obs_value)[:, None], leakage, padded, pcov,
-        prior_prec[None],
+        diag_blocks.reshape(dl * n, S), off_blocks.reshape(dl * n, S), vert, obs_bary, covariates,
+        slot_weight, obs_value, leakage, probes, probes_cov, prior_prec[None],
     )
     return (jnp.moveaxis(field, 0, 1), out_cov)
 

time: 158 us -> 115 us (0.73)
  Pallas kernels: 141 us -> 105 us
  local copies, waits for them, and re-layouts: 12.6 us -> 6.26 us
    pallas_call x1, Pallas kernels: 141 us -> 105 us  [on_device(): pl.pallas_call(functools.partial(kernel, D, B, R, dl, n, J, C), out_shape...]
    unnamed x6 -> x4, local copies, waits for them, and re-layouts: 6.97 us -> 4.52 us
where the time goes in v2:
time: 115 us; the launch traced here: 114 us
  Pallas kernels  105 us (91%)
  local copies, waits for them, and re-layouts  6.26 us (5%)
  other arithmetic  2.03 us (2%)
    pallas_call x1, Pallas kernels, on_device(): pl.pallas_call(functools.partial(kernel, D, B, R, dl, n, J, C), out_shape...  105 us
    unnamed x4, local copies, waits for them, and re-layouts  4.52 us

profile of v2, /device:TPU:0, one launch (start us, length us, event | category | flops | bytes accessed | tf_op | source)
XLA Modules:
  0.0 114.4 jit_solution(10146516179697900107)
XLA Ops:
  0.6 1.7 %copy.15 = s32[3,5116]{0,1:T(8,128)S(1)} copy(s32[3,5116]{1,0:T(4,128)} %param.22) | data formatting | bytes 122784 | tf_op args[9]
  2.3 0.7 fusion
  3.0 1.0 gather_fusion
  4.0 0.7 copy.18
  4.7 1.3 %compare_select_fusion.1.slotw = f32[2,256]{1,0:T(2,128)} fusion(f32[2,256]{1,0:T(2,128)} %param.19, s32[256]{0:T(256)S(1)} %iota_add_fusion, s32[2]{0:T(128)} %param.16), kind=kLoop, calls=%fused_computation.3 | loop fusion | flops 1024 | bytes 5128 | tf_op jit(solution)/shard_map/jit(_where)/select_n | solution.py:413
  6.1 105.5 %shard_map.140 = (f32[2,16,640]{2,1,0:T(8,128)}, f32[16,64]{1,0:T(8,128)}) custom-call(f32[1280,2560]{1,0:T(8,128)} %bitcast.9, f32[1280,2560]{1,0:T(8,128)} %bitcast.10, s32[3,2,256]{2,1,0:T(2,128)} %bitcast.13, f32[3,2,256]{2,1,0:T(2,128)} %bary.1, f32[64,2,256]{2,1,0:T(2,128)} %cov_in.1, f32[2,256]{1,0:T(2,128)} %compare_select_fusion.1.slotw, ...), custom_call_target="tpu_custom_call" | custom-call | tf_op jit(solution)/shard_map/pallas_call | solution.py:441
  111.6 1.6 %copy.17 = f32[16,2,640]{2,1,0:T(2,128)} copy(f32[16,2,640]{2,0,1:T(8,128)} %bitcast.12) | data formatting | bytes 163840
  113.1 1.3 %copy.21 = f32[16,64]{1,0:T(8,128)} copy(f32[16,64]{1,0:T(8,128)} %get-tuple-element.11) | data formatting | bytes 8192
  (3 shorter events, 0.0 us)

commit v3 on v2

--- a/solution.py
+++ b/solution.py
@@ -36,7 +36,7 @@
     field_out, cov_out,
     mhi, mlo, ahi, alo, stage, stage_sem,
     dacc, own_dom, leak_all, dom_all, g_snd, g_rcv, gc_snd, gc_rcv, gcd_snd, gcd_rcv,
-    cov, rawd, rawb, x_snd, x_rcv, resid, pre, pre_rcv, npart, n_rcv, ncol, nb_rcv, pre_own, pre_full,
+    cov, sol, rawd, rawb, x_snd, x_rcv, resid, pre, pre_rcv, npart, n_rcv, ncol, nb_rcv, pre_own, pre_full,
     dirs, dhl, ohl, part, behind, ahead, p_snd, p_rcv, q_snd, q_rcv, cc, cc_b, cs, cc_d, stepd,
     sem_blk, sem_day, sem_next,
 ):
@@ -383,7 +383,10 @@
         step = norm_now / curvature
         for t in range(dl):
             add = step * dirs[it, me_b, t]
-            field_out[t] = add if it == 0 else field_out[t] + add
+            ahead[t] = add if it == 0 else sol[t] + add
+            sol[t] = ahead[t]
+            if last:
+                field_out[:, t, :] = ahead[t]
         sol_cov = sol_cov + step * dir_cov
         if not last:
             resid_cov = resid_cov - step * image_cov
@@ -422,7 +425,7 @@
         vm((dl, 8, S), F32), vm((dl, n), F32), vm((D, dl, n), F32), vm((D, dl, n), F32),
         vm((B, dl, 8, n), F32), vm((B, dl, 8, n), F32), vm((8, 128), F32), vm((B, 8, 128), F32),
         vm((8, 128), F32), vm((D, 8, 128), F32),
-        vm((dl, C, J), F32), vm((dl, R, S), F32), vm((dl, R, S), F32),
+        vm((dl, C, J), F32), vm((dl, R, n), F32), vm((dl, R, S), F32), vm((dl, R, S), F32),
         vm((D, dl, Rd, n), F32), vm((ITERS, D, dl, Rd, n), F32), vm((D, dl, Rd, n), F32),
         vm((D * dl + 1, Rd, n), F32), vm((ITERS, D, dl + 1, Rd, n), F32),
         vm((Rd, 128), F32), vm((ITERS, D, Rd, 128), F32), vm((R, 128), F32),
@@ -440,7 +443,7 @@
     inside = pl.BlockSpec(memory_space=pltpu.VMEM)
     field, out_cov = pl.pallas_call(
         functools.partial(kernel, D, B, R, dl, n, J, C),
-        out_shape=(jax.ShapeDtypeStruct((dl, R, n), F32), jax.ShapeDtypeStruct((R, C), F32)),
+        out_shape=(jax.ShapeDtypeStruct((R, dl, n), F32), jax.ShapeDtypeStruct((R, C), F32)),
         in_specs=[anywhere] * 2 + [inside] * 9,
         out_specs=(inside, inside),
         scratch_shapes=scratch,
@@ -451,7 +454,7 @@
         diag_blocks.reshape(dl * n, S), off_blocks.reshape(dl * n, S), vert, obs_bary, covariates,
         slot_weight, obs_value, leakage, probes, probes_cov, prior_prec[None],
     )
-    return (jnp.moveaxis(field, 0, 1), out_cov)
+    return (field, out_cov)
 
 
 def solution(mesh):

time: 115 us -> 115 us (level)
  no operation moved by 1% of the time
where the time goes in v3:
time: 115 us; the launch traced here: 114 us
  Pallas kernels  105 us (91%)
  local copies, waits for them, and re-layouts  6.22 us (5%)
  other arithmetic  2.03 us (2%)
    pallas_call x1, Pallas kernels, on_device(): pl.pallas_call(functools.partial(kernel, D, B, R, dl, n, J, C), out_shape...  105 us
    unnamed x4, local copies, waits for them, and re-layouts  4.48 us

profile of v3, /device:TPU:0, one launch (start us, length us, event | category | flops | bytes accessed | tf_op | source)
XLA Modules:
  0.0 114.2 jit_solution(6248489742185918787)
XLA Ops:
  0.6 1.7 %copy.15 = s32[3,5116]{0,1:T(8,128)S(1)} copy(s32[3,5116]{1,0:T(4,128)} %param.22) | data formatting | bytes 122784 | tf_op args[9]
  2.3 0.7 fusion
  3.0 1.0 gather_fusion
  4.0 0.7 copy.17
  4.7 1.3 %compare_select_fusion.1.slotw = f32[2,256]{1,0:T(2,128)} fusion(f32[2,256]{1,0:T(2,128)} %param.19, s32[256]{0:T(256)S(1)} %iota_add_fusion, s32[2]{0:T(128)} %param.16), kind=kLoop, calls=%fused_computation.3 | loop fusion | flops 1024 | bytes 5128 | tf_op jit(solution)/shard_map/jit(_where)/select_n | solution.py:416
  6.1 105.3 %shard_map.140 = (f32[16,2,640]{2,1,0:T(2,128)}, f32[16,64]{1,0:T(8,128)}) custom-call(f32[1280,2560]{1,0:T(8,128)} %bitcast.8, f32[1280,2560]{1,0:T(8,128)} %bitcast.9, s32[3,2,256]{2,1,0:T(2,128)} %bitcast.11, f32[3,2,256]{2,1,0:T(2,128)} %bary.1, f32[64,2,256]{2,1,0:T(2,128)} %cov_in.1, f32[2,256]{1,0:T(2,128)} %compare_select_fusion.1.slotw, ...), custom_call_target="tpu_custom_call" | custom-call | tf_op jit(solution)/shard_map/pallas_call | solution.py:444
  111.4 1.5 %copy.21 = f32[16,2,640]{2,1,0:T(2,128)} copy(f32[16,2,640]{2,1,0:T(2,128)} %get-tuple-element.4) | data formatting | bytes 163840
  112.9 1.3 %copy.22 = f32[16,64]{1,0:T(8,128)} copy(f32[16,64]{1,0:T(8,128)} %get-tuple-element.5) | data formatting | bytes 8192
  (3 shorter events, 0.0 us)
